TPU v7x, 32 devices: a whole 2x2x4 slice. The times are simulated.
32 devices in a mesh: macro: 8 (over z, x), rep: 4 (over y, core).
Axes of the slice: x: 2, y: 2, z: 4, core: 2. Of those that a mesh axis runs over, the one named last changes fastest.
Arguments:
- u_old: float32 [4096], P('macro'), may hold values from -1 to 1
- coarse_kinetic_speed: float32 [4096], P('macro'), may hold values from 0.2 to 3
- micro_spreading_coefficient: float32 [4096], P('macro'), may hold values from 0.08 to 0.4
- micro_seed: int32 [4, 4096, 256], P('rep', 'macro'), may hold values from 0 to 1073741823
Outputs:
- new_state: float32 [4096], P('macro')
All inputs are finite; a program needn't handle non-finite values.
Results may differ from a plain program's by a relative error of at most 0.0001.
Values sent between devices are 32-bit elements; how exact they have to be, the bound alone decides.
A program may use at most 64 MiB of HBM per device.

v0:
```python
import math
import jax
import jax.numpy as jnp
from jax import lax
from jax.sharding import PartitionSpec as P

STEPS = 8
ITERS = 4
noise_amp = 1.0
micro_dt = 0.02
proj_step = 0.25
fd_step = 0.01
seed_scale = 2.0 ** (-30)


def with_halo(cells, sides, width):
    for axis, dim in sides:
        count = lax.axis_size(axis)
        ends = count - 1
        head = lax.slice_in_dim(cells, 0, width, axis=dim)
        tail = lax.slice_in_dim(cells, cells.shape[dim] - width, cells.shape[dim], axis=dim)
        cells = jnp.concatenate(
            [
                lax.ppermute(tail, axis, [(i, (i + 1) % count) for i in range(ends)]),
                cells,
                lax.ppermute(head, axis, [((i + 1) % count, i) for i in range(ends)]),
            ],
            axis=dim,
        )
    return cells


def lifted(padded_density, cells):
    left = padded_density[:-2]
    centre = padded_density[1:-1]
    right = padded_density[2:]
    slope = 0.5 * (right - left)
    bend = 0.5 * (right - 2.0 * centre + left)
    place = (jnp.arange(cells).astype(jnp.float32) + 0.5) / cells - 0.5
    inside = (
        centre[:, None] + slope[:, None] * place[None, :] + bend[:, None] * (place * place)[None, :]
    )
    edge = 0.5 + 0.5 / cells
    ghost_left = centre - slope * edge + bend * edge * edge
    ghost_right = centre + slope * edge + bend * edge * edge
    return (inside, ghost_left, ghost_right)


def ensemble_aggregate(padded_density, pointwise_kinetic_speed, spreading_current, stochastic_kick):
    inside, ghost_left, ghost_right = lifted(padded_density, stochastic_kick.shape[2])
    start = inside[None] + stochastic_kick
    left_col = ghost_left[None, :, None]
    right_col = ghost_right[None, :, None]
    kappa = spreading_current[None, :, None]
    growth = micro_dt * pointwise_kinetic_speed[None, :, None]
    state = start
    for step in range(STEPS):
        upper = jnp.concatenate([state[:, :, 1:], right_col], axis=2)
        lower = jnp.concatenate([left_col, state[:, :, :-1]], axis=2)
        state = (
            state + kappa * (upper + lower - 2.0 * state) + growth * (state - state * state * state)
        )
    return jnp.sum(state - start, axis=(0, 2))


def least_squares(hess, beta, iters):
    target = [beta] + [beta * 0.0 for index in range(iters)]
    cosines = []
    sines = []
    upper = []
    for col_index in range(iters):
        column = [hess[row][col_index] for row in range(col_index + 2)]
        for row in range(col_index):
            first = column[row]
            second = column[row + 1]
            column[row] = cosines[row] * first + sines[row] * second
            column[row + 1] = -sines[row] * first + cosines[row] * second
        radius = jnp.sqrt(
            column[col_index] * column[col_index] + column[col_index + 1] * column[col_index + 1]
        )
        cosine = column[col_index] / radius
        sine = column[col_index + 1] / radius
        cosines.append(cosine)
        sines.append(sine)
        column[col_index] = radius
        upper.append(column[: col_index + 1])
        head = target[col_index]
        target[col_index] = cosine * head
        target[col_index + 1] = -sine * head
    solved = [None] * iters
    for row in range(iters - 1, -1, -1):
        acc = target[row]
        for later in range(row + 1, iters):
            acc = acc - upper[later][row] * solved[later]
        solved[row] = acc / upper[row][row]
    return solved


def per_device(u_old, coarse_kinetic_speed, micro_spreading_coefficient, micro_seed):
    local = u_old.shape[0]
    groups = lax.axis_size("rep")
    fluctuation_amplitude = 1.0 / (
        micro_seed.shape[0] * groups * micro_seed.shape[2] * STEPS * micro_dt
    )
    delta = fd_step * math.sqrt(lax.axis_size("macro") * local)
    stochastic_kick = noise_amp * (micro_seed.astype(jnp.float32) * seed_scale - 0.5)

    def drift(species_density):
        padded_density = with_halo(species_density, (("macro", 0),), 1)
        increment_parts = ensemble_aggregate(
            padded_density, coarse_kinetic_speed, micro_spreading_coefficient, stochastic_kick
        )
        summed = lax.psum(increment_parts, "rep")
        return summed * fluctuation_amplitude

    def inner(values):
        return lax.psum(values, "macro")

    f_old = drift(u_old)
    u_start = u_old + proj_step * f_old
    f_start = drift(u_start)
    resid = -(u_start - u_old - proj_step * f_start)
    beta = jnp.sqrt(inner(jnp.sum(resid * resid)))
    basis = [resid / beta]
    hess = [[None] * ITERS for row in range(ITERS + 1)]
    for col_index in range(ITERS):
        probe = basis[col_index]
        image = probe - proj_step * (drift(u_start + delta * probe) - f_start) / delta
        pieces = [jnp.sum(basis[row] * image) for row in range(col_index + 1)]
        pieces.append(jnp.sum(image * image))
        dots = inner(jnp.stack(pieces))
        for row in range(col_index + 1):
            hess[row][col_index] = dots[row]
            image = image - dots[row] * basis[row]
        coeff_sq = jnp.sum(dots[: col_index + 1] * dots[: col_index + 1])
        length = jnp.sqrt(jnp.maximum(dots[col_index + 1] - coeff_sq, 0.0))
        hess[col_index + 1][col_index] = length
        basis.append(image / length)
    coeffs = least_squares(hess, beta, ITERS)
    result = u_start
    for col_index in range(ITERS):
        result = result + coeffs[col_index] * basis[col_index]
    return result


def solution(mesh):
    placed = (P("macro"), P("macro"), P("macro"), P("rep", "macro", None))
    return jax.shard_map(
        per_device, mesh=mesh, in_specs=placed, out_specs=P("macro"), check_vma=False
    )
```

profile of v0, /device:TPU:0, one launch (start us, length us, event | category | flops | bytes accessed | tf_op | source)
XLA Modules:
  0.0 276.7 jit_solution(14354860609766797719)
XLA Ops:
  0.0 1.4 fusion.354
  1.4 1.4 collective-permute-start
  2.8 6.0 %collective-permute-start.1 = (f32[1]{0:T(128)}, f32[1]{0:T(128)}, u32[]{:S(2)}, u32[]{:S(2)}) collective-permute-start(f32[1]{0:T(128)} %get-tuple-element.172), channel_id=1, source_target_pairs={{0,4},{4,8},{8,12},{12,16},{16,20},{20,24},{24,28},{1,5},{5,9},{9,... | collective-permute-start | bytes 20 | tf_op jit(solution)/shard_map/ppermute | solution.py:24
  8.9 0.8 collective-permute-done.1
  9.7 1.3 pad_maximum_fusion.96
  11.0 1.3 add_add_fusion.5
  18.2 0.8 fusion.17
  18.9 6.5 %psum.77 = f32[512]{0:T(512)S(1)} all-reduce(f32[512]{0:T(512)S(1)} %fusion.17), channel_id=1, replica_groups=mesh['macro'=8,'rep'=4] {'rep'}, use_global_device_ids=true, to_apply=%region_1.0 | all-reduce | flops 512 | bytes 4096 | tf_op jit(solution)/shard_map/psum | solution.py:113
  26.1 1.3 collective-permute-start.2
  27.4 5.2 %collective-permute-start.3 = (f32[1]{0:T(128)}, f32[1]{0:T(128)}, u32[]{:S(2)}, u32[]{:S(2)}) collective-permute-start(f32[1]{0:T(128)} %get-tuple-element.168), channel_id=1, source_target_pairs={{0,4},{4,8},{8,12},{12,16},{16,20},{20,24},{24,28},{1,5},{5,9},{9,... | collective-permute-start | bytes 20 | tf_op jit(solution)/shard_map/ppermute | solution.py:24
  32.6 0.8 collective-permute-done.3
  33.4 1.3 pad_maximum_fusion.98
  40.1 0.8 fusion.35
  40.8 5.9 %psum.78 = f32[512]{0:T(512)S(1)} all-reduce(f32[512]{0:T(512)S(1)} %fusion.35), channel_id=1, replica_groups=mesh['macro'=8,'rep'=4] {'rep'}, use_global_device_ids=true, to_apply=%region_3.0 | all-reduce | flops 512 | bytes 4096 | tf_op jit(solution)/shard_map/psum | solution.py:113
  47.4 25.6 %psum.79 = f32[]{:T(128)} all-reduce(f32[]{:T(128)} %multiply_reduce_fusion.14), channel_id=1, replica_groups=mesh['macro'=8,'rep'=4] {'macro'}, use_global_device_ids=true, to_apply=%region_5.0 | all-reduce | flops 1 | bytes 8 | tf_op jit(solution)/shard_map/psum | solution.py:117
  74.4 1.3 collective-permute-start.4
  75.7 5.1 %collective-permute-start.5 = (f32[1]{0:T(128)}, f32[1]{0:T(128)}, u32[]{:S(2)}, u32[]{:S(2)}) collective-permute-start(f32[1]{0:T(128)} %get-tuple-element.164), channel_id=1, source_target_pairs={{0,4},{4,8},{8,12},{12,16},{16,20},{20,24},{24,28},{1,5},{5,9},{9,... | collective-permute-start | bytes 20 | tf_op jit(solution)/shard_map/ppermute | solution.py:24
  80.8 0.8 collective-permute-done.5
  81.6 1.3 pad_maximum_fusion.100
  88.3 0.8 fusion.53
  89.0 5.7 %psum.80 = f32[512]{0:T(512)S(1)} all-reduce(f32[512]{0:T(512)S(1)} %fusion.53), channel_id=1, replica_groups=mesh['macro'=8,'rep'=4] {'rep'}, use_global_device_ids=true, to_apply=%region_7.0 | all-reduce | flops 512 | bytes 4096 | tf_op jit(solution)/shard_map/psum | solution.py:113
  95.4 1.4 pad_maximum_fusion.108
  96.8 19.5 %psum.81 = f32[2]{0:T(128)S(1)} all-reduce(f32[2]{0:T(128)S(1)} %pad_maximum_fusion.108), channel_id=1, replica_groups=mesh['macro'=8,'rep'=4] {'macro'}, use_global_device_ids=true, to_apply=%region_10.0 | all-reduce | flops 2 | bytes 16 | tf_op jit(solution)/shard_map/psum | solution.py:117
  122.3 1.3 collective-permute-start.6
  123.6 5.1 %collective-permute-start.7 = (f32[1]{0:T(128)}, f32[1]{0:T(128)}, u32[]{:S(2)}, u32[]{:S(2)}) collective-permute-start(f32[1]{0:T(128)} %get-tuple-element.160), channel_id=1, source_target_pairs={{0,4},{4,8},{8,12},{12,16},{16,20},{20,24},{24,28},{1,5},{5,9},{9,... | collective-permute-start | bytes 20 | tf_op jit(solution)/shard_map/ppermute | solution.py:24
  128.7 0.8 collective-permute-done.7
  129.5 1.3 pad_maximum_fusion.102
  137.0 5.7 %psum.82 = f32[512]{0:T(512)S(1)} all-reduce(f32[512]{0:T(512)S(1)} %fusion.71), channel_id=1, replica_groups=mesh['macro'=8,'rep'=4] {'rep'}, use_global_device_ids=true, to_apply=%region_12.0 | all-reduce | flops 512 | bytes 4096 | tf_op jit(solution)/shard_map/psum | solution.py:113
  143.4 2.0 pad_maximum_fusion.109
  145.3 19.5 %psum.83 = f32[3]{0:T(128)S(1)} all-reduce(f32[3]{0:T(128)S(1)} %pad_maximum_fusion.109), channel_id=1, replica_groups=mesh['macro'=8,'rep'=4] {'macro'}, use_global_device_ids=true, to_apply=%region_16.0 | all-reduce | flops 3 | bytes 24 | tf_op jit(solution)/shard_map/psum | solution.py:117
  170.2 1.3 multiply_add_fusion.3
  172.2 1.3 collective-permute-start.8
  173.5 5.1 %collective-permute-start.9 = (f32[1]{0:T(128)}, f32[1]{0:T(128)}, u32[]{:S(2)}, u32[]{:S(2)}) collective-permute-start(f32[1]{0:T(128)} %get-tuple-element.156), channel_id=1, source_target_pairs={{0,4},{4,8},{8,12},{12,16},{16,20},{20,24},{24,28},{1,5},{5,9},{9,... | collective-permute-start | bytes 20 | tf_op jit(solution)/shard_map/ppermute | solution.py:24
  178.5 0.8 collective-permute-done.9
  179.4 1.3 pad_maximum_fusion.104
  186.1 0.8 fusion.89
  186.8 5.7 %psum.84 = f32[512]{0:T(512)S(1)} all-reduce(f32[512]{0:T(512)S(1)} %fusion.89), channel_id=1, replica_groups=mesh['macro'=8,'rep'=4] {'rep'}, use_global_device_ids=true, to_apply=%region_19.0 | all-reduce | flops 512 | bytes 4096 | tf_op jit(solution)/shard_map/psum | solution.py:113
  193.2 2.6 pad_maximum_fusion.110
  195.8 19.5 %psum.85 = f32[4]{0:T(128)S(1)} all-reduce(f32[4]{0:T(128)S(1)} %pad_maximum_fusion.110), channel_id=1, replica_groups=mesh['macro'=8,'rep'=4] {'macro'}, use_global_device_ids=true, to_apply=%region_24.0 | all-reduce | flops 4 | bytes 32 | tf_op jit(solution)/shard_map/psum | solution.py:117
  221.9 1.9 multiply_add_fusion.2
  224.4 1.3 collective-permute-start.10
  225.7 5.1 %collective-permute-start.11 = (f32[1]{0:T(128)}, f32[1]{0:T(128)}, u32[]{:S(2)}, u32[]{:S(2)}) collective-permute-start(f32[1]{0:T(128)} %get-tuple-element.152), channel_id=1, source_target_pairs={{0,4},{4,8},{8,12},{12,16},{16,20},{20,24},{24,28},{1,5},{5,9},{9,... | collective-permute-start | bytes 20 | tf_op jit(solution)/shard_map/ppermute | solution.py:24
  230.8 0.8 collective-permute-done.11
  231.6 1.3 pad_maximum_fusion.106
  238.3 0.8 fusion.107
  239.1 5.7 %psum.86 = f32[512]{0:T(512)S(1)} all-reduce(f32[512]{0:T(512)S(1)} %fusion.107), channel_id=1, replica_groups=mesh['macro'=8,'rep'=4] {'rep'}, use_global_device_ids=true, to_apply=%region_27.0 | all-reduce | flops 512 | bytes 4096 | tf_op jit(solution)/shard_map/psum | solution.py:113
  245.5 3.2 %stack.71 = f32[5]{0:T(128)S(1)} concatenate(f32[1]{0:T(128)} %bitcast.30, f32[1]{0:T(128)} %bitcast.31, f32[1]{0:T(128)} %bitcast.32, f32[1]{0:T(128)} %bitcast.33, f32[1]{0:T(128)} %bitcast.34), dimensions={0} | concatenate | bytes 40 | tf_op jit(solution)/shard_map/stack | solution.py:131
  248.7 19.5 %psum.87 = f32[5]{0:T(128)S(1)} all-reduce(f32[5]{0:T(128)S(1)} %stack.71), channel_id=1, replica_groups=mesh['macro'=8,'rep'=4] {'macro'}, use_global_device_ids=true, to_apply=%region_33.0 | all-reduce | flops 5 | bytes 40 | tf_op jit(solution)/shard_map/psum | solution.py:117
  (151 shorter events, 46.1 us)
Async XLA Ops:
  1.4 7.5 %copy-start.3 = (f32[512]{0:T(512)S(1)}, f32[512]{0:T(512)}, u32[]{:S(2)}) copy-start(f32[512]{0:T(512)} %param.5) | copy-start | bytes 6148
  1.4 7.5 %collective-permute-start = (f32[1]{0:T(128)}, f32[1]{0:T(128)}, u32[]{:S(2)}, u32[]{:S(2)}) collective-permute-start(f32[1]{0:T(128)} %get-tuple-element.171), channel_id=1, source_target_pairs={{4,0},{8,4},{12,8},{16,12},{20,16},{24,20},{28,24},{5,1},{9,5},{13... | collective-permute-start | bytes 20 | tf_op jit(solution)/shard_map/ppermute | solution.py:26
  2.8 6.8 %collective-permute-start.1 = (f32[1]{0:T(128)}, f32[1]{0:T(128)}, u32[]{:S(2)}, u32[]{:S(2)}) collective-permute-start(f32[1]{0:T(128)} %get-tuple-element.172), channel_id=1, source_target_pairs={{0,4},{4,8},{8,12},{12,16},{16,20},{20,24},{24,28},{1,5},{5,9},{9,... | collective-permute-start | bytes 20 | tf_op jit(solution)/shard_map/ppermute | solution.py:24
  8.9 0.8 copy-start.2
  12.5 1.0 copy-start
  12.9 0.7 copy-start.1
  26.1 6.5 %collective-permute-start.2 = (f32[1]{0:T(128)}, f32[1]{0:T(128)}, u32[]{:S(2)}, u32[]{:S(2)}) collective-permute-start(f32[1]{0:T(128)} %get-tuple-element.167), channel_id=1, source_target_pairs={{4,0},{8,4},{12,8},{16,12},{20,16},{24,20},{28,24},{5,1},{9,5},{13... | collective-permute-start | bytes 20 | tf_op jit(solution)/shard_map/ppermute | solution.py:26
  27.4 6.0 %collective-permute-start.3 = (f32[1]{0:T(128)}, f32[1]{0:T(128)}, u32[]{:S(2)}, u32[]{:S(2)}) collective-permute-start(f32[1]{0:T(128)} %get-tuple-element.168), channel_id=1, source_target_pairs={{0,4},{4,8},{8,12},{12,16},{16,20},{20,24},{24,28},{1,5},{5,9},{9,... | collective-permute-start | bytes 20 | tf_op jit(solution)/shard_map/ppermute | solution.py:24
  74.4 6.4 %collective-permute-start.4 = (f32[1]{0:T(128)}, f32[1]{0:T(128)}, u32[]{:S(2)}, u32[]{:S(2)}) collective-permute-start(f32[1]{0:T(128)} %get-tuple-element.163), channel_id=1, source_target_pairs={{4,0},{8,4},{12,8},{16,12},{20,16},{24,20},{28,24},{5,1},{9,5},{13... | collective-permute-start | bytes 20 | tf_op jit(solution)/shard_map/ppermute | solution.py:26
  75.7 5.9 %collective-permute-start.5 = (f32[1]{0:T(128)}, f32[1]{0:T(128)}, u32[]{:S(2)}, u32[]{:S(2)}) collective-permute-start(f32[1]{0:T(128)} %get-tuple-element.164), channel_id=1, source_target_pairs={{0,4},{4,8},{8,12},{12,16},{16,20},{20,24},{24,28},{1,5},{5,9},{9,... | collective-permute-start | bytes 20 | tf_op jit(solution)/shard_map/ppermute | solution.py:24
  122.3 6.4 %collective-permute-start.6 = (f32[1]{0:T(128)}, f32[1]{0:T(128)}, u32[]{:S(2)}, u32[]{:S(2)}) collective-permute-start(f32[1]{0:T(128)} %get-tuple-element.159), channel_id=1, source_target_pairs={{4,0},{8,4},{12,8},{16,12},{20,16},{24,20},{28,24},{5,1},{9,5},{13... | collective-permute-start | bytes 20 | tf_op jit(solution)/shard_map/ppermute | solution.py:26
  123.6 5.9 %collective-permute-start.7 = (f32[1]{0:T(128)}, f32[1]{0:T(128)}, u32[]{:S(2)}, u32[]{:S(2)}) collective-permute-start(f32[1]{0:T(128)} %get-tuple-element.160), channel_id=1, source_target_pairs={{0,4},{4,8},{8,12},{12,16},{16,20},{20,24},{24,28},{1,5},{5,9},{9,... | collective-permute-start | bytes 20 | tf_op jit(solution)/shard_map/ppermute | solution.py:24
  172.2 6.4 %collective-permute-start.8 = (f32[1]{0:T(128)}, f32[1]{0:T(128)}, u32[]{:S(2)}, u32[]{:S(2)}) collective-permute-start(f32[1]{0:T(128)} %get-tuple-element.155), channel_id=1, source_target_pairs={{4,0},{8,4},{12,8},{16,12},{20,16},{24,20},{28,24},{5,1},{9,5},{13... | collective-permute-start | bytes 20 | tf_op jit(solution)/shard_map/ppermute | solution.py:26
  173.5 5.9 %collective-permute-start.9 = (f32[1]{0:T(128)}, f32[1]{0:T(128)}, u32[]{:S(2)}, u32[]{:S(2)}) collective-permute-start(f32[1]{0:T(128)} %get-tuple-element.156), channel_id=1, source_target_pairs={{0,4},{4,8},{8,12},{12,16},{16,20},{20,24},{24,28},{1,5},{5,9},{9,... | collective-permute-start | bytes 20 | tf_op jit(solution)/shard_map/ppermute | solution.py:24
  224.4 6.4 %collective-permute-start.10 = (f32[1]{0:T(128)}, f32[1]{0:T(128)}, u32[]{:S(2)}, u32[]{:S(2)}) collective-permute-start(f32[1]{0:T(128)} %get-tuple-element.151), channel_id=1, source_target_pairs={{4,0},{8,4},{12,8},{16,12},{20,16},{24,20},{28,24},{5,1},{9,5},{13... | collective-permute-start | bytes 20 | tf_op jit(solution)/shard_map/ppermute | solution.py:26
  225.7 5.9 %collective-permute-start.11 = (f32[1]{0:T(128)}, f32[1]{0:T(128)}, u32[]{:S(2)}, u32[]{:S(2)}) collective-permute-start(f32[1]{0:T(128)} %get-tuple-element.152), channel_id=1, source_target_pairs={{0,4},{4,8},{8,12},{12,16},{16,20},{20,24},{24,28},{1,5},{5,9},{9,... | collective-permute-start | bytes 20 | tf_op jit(solution)/shard_map/ppermute | solution.py:24
where the time goes:
time: 278 us; the launch traced here: 277 us
  blocking collectives  139 us (50%)
  other arithmetic  49.8 us (18%)
  starting transfers between devices  39.4 us (14%)
  local copies, waits for them, and re-layouts  22.8 us (8%)
  between operations  21.2 us (8%)
  waiting for transfers between devices  4.81 us (2%)
    psum x5, blocking collectives, inner(): return lax.psum(values, 'macro')  104 us
    psum x6, blocking collectives, drift(): summed = lax.psum(increment_parts, 'rep')  35.1 us
    ppermute x6, starting transfers between devices, with_halo(): lax.ppermute(tail, axis, [(i, (i + 1) % count) for i in range(ends)])  31.6 us
    add x42, other arithmetic, ensemble_aggregate(): state + kappa * (upper + lower - 2.0 * state)  18.8 us
    slice x48, local copies, waits for them, and re-layouts, ensemble_aggregate(): lower = jnp.concatenate([left_col, state[:, :, :-1]], axis=2)  9.65 us
    ppermute x6, starting transfers between devices, with_halo(): lax.ppermute(head, axis, [((i + 1) % count, i) for i in range(ends)])  7.81 us
    concatenate x6, other arithmetic, with_halo(): jnp.concatenate([lax.ppermute(tail, axis, [(i, (i + 1) % count) for i in...  7.59 us
    another operation x3, other arithmetic, per_device(): dots = inner(jnp.stack(pieces))  5.98 us
  transfers between devices with their start and end apart: 12, of which 6 were waited for; matrix products, arithmetic and copies ran while one was open for 0% of the time, Pallas kernels for 0%

commit v1 on v0

--- a/solution.py
+++ b/solution.py
@@ -110,7 +110,13 @@
         increment_parts = ensemble_aggregate(
             padded_density, coarse_kinetic_speed, micro_spreading_coefficient, stochastic_kick
         )
-        summed = lax.psum(increment_parts, "rep")
+        size = lax.axis_size("rep")
+        summed, reach = (increment_parts, 1)
+        while reach < size:
+            summed = summed + lax.ppermute(
+                summed, "rep", [(i_2, i_2 ^ reach) for i_2 in range(size)]
+            )
+            reach = 2 * reach
         return summed * fluctuation_amplitude
 
     def inner(values):

time: 278 us -> 270 us (0.971)
  blocking collectives: 139 us -> 103 us
  waiting for transfers between devices: 4.81 us -> 21.8 us
  starting transfers between devices: 39.4 us -> 50.4 us
    psum x6 -> x0, blocking collectives: 35.1 us -> none  [drift(): summed = lax.psum(increment_parts, 'rep')]
    ppermute x0 -> x12, waiting for transfers between devices: none -> 16.7 us  [drift(): lax.ppermute(summed, 'rep', [(i_2, i_2 ^ reach) for i_2 in range(size)])]
    ppermute x0 -> x12, starting transfers between devices: none -> 10.1 us  [drift(): lax.ppermute(summed, 'rep', [(i_2, i_2 ^ reach) for i_2 in range(size)])]
  transfers between devices with their start and end apart: 12 -> 24, of which waited for: 6 -> 17; matrix products, arithmetic and copies ran while one was open for 0% -> 0% of each run, Pallas kernels for 0% -> 0%
where the time goes in v1:
time: 270 us; the launch traced here: 269 us
  blocking collectives  103 us (38%)
  starting transfers between devices  50.4 us (19%)
  other arithmetic  50.1 us (19%)
  local copies, waits for them, and re-layouts  22.5 us (8%)
  waiting for transfers between devices  21.8 us (8%)
  between operations  21.3 us (8%)
    psum x5, blocking collectives, inner(): return lax.psum(values, 'macro')  103 us
    ppermute x6, starting transfers between devices, with_halo(): lax.ppermute(tail, axis, [(i, (i + 1) % count) for i in range(ends)])  32.6 us
    add x42, other arithmetic, ensemble_aggregate(): state + kappa * (upper + lower - 2.0 * state)  18.7 us
    ppermute x12, waiting for transfers between devices, drift(): lax.ppermute(summed, 'rep', [(i_2, i_2 ^ reach) for i_2 in range(size)])  16.7 us
    ppermute x12, starting transfers between devices, drift(): lax.ppermute(summed, 'rep', [(i_2, i_2 ^ reach) for i_2 in range(size)])  10.1 us
    slice x48, local copies, waits for them, and re-layouts, ensemble_aggregate(): lower = jnp.concatenate([left_col, state[:, :, :-1]], axis=2)  9.65 us
    concatenate x6, other arithmetic, with_halo(): jnp.concatenate([lax.ppermute(tail, axis, [(i, (i + 1) % count) for i in...  7.98 us
    ppermute x6, starting transfers between devices, with_halo(): lax.ppermute(head, axis, [((i + 1) % count, i) for i in range(ends)])  7.81 us
  transfers between devices with their start and end apart: 24, of which 17 were waited for; matrix products, arithmetic and copies ran while one was open for 0% of the time, Pallas kernels for 0%

profile of v1, /device:TPU:0, one launch (start us, length us, event | category | flops | bytes accessed | tf_op | source)
XLA Modules:
  0.0 269.0 jit_solution(8321448398449658509)
XLA Ops:
  0.0 1.4 fusion.354
  1.4 1.4 collective-permute-start
  2.8 6.1 %collective-permute-start.1 = (f32[1]{0:T(128)}, f32[1]{0:T(128)}, u32[]{:S(2)}, u32[]{:S(2)}) collective-permute-start(f32[1]{0:T(128)} %get-tuple-element.175), channel_id=1, source_target_pairs={{0,4},{4,8},{8,12},{12,16},{16,20},{20,24},{24,28},{1,5},{5,9},{9,... | collective-permute-start | bytes 20 | tf_op jit(solution)/shard_map/ppermute | solution.py:24
  9.8 1.3 pad_maximum_fusion.96
  11.2 1.3 add_add_fusion.5
  19.2 1.1 collective-permute-done.2
  20.3 2.0 collective-permute-start.3
  22.4 1.6 collective-permute-done.3
  24.5 1.3 collective-permute-start.4
  25.8 6.0 %collective-permute-start.5 = (f32[1]{0:T(128)}, f32[1]{0:T(128)}, u32[]{:S(2)}, u32[]{:S(2)}) collective-permute-start(f32[1]{0:T(128)} %get-tuple-element.171), channel_id=1, source_target_pairs={{0,4},{4,8},{8,12},{12,16},{16,20},{20,24},{24,28},{1,5},{5,9},{9,... | collective-permute-start | bytes 20 | tf_op jit(solution)/shard_map/ppermute | solution.py:24
  32.7 1.3 pad_maximum_fusion.98
  40.4 1.1 collective-permute-done.6
  41.5 1.5 collective-permute-start.7
  43.0 2.1 collective-permute-done.7
  45.7 25.6 %psum.35 = f32[]{:T(128)} all-reduce(f32[]{:T(128)} %get-tuple-element.30), channel_id=1, replica_groups=mesh['macro'=8,'rep'=4] {'macro'}, use_global_device_ids=true, to_apply=%region_3.0 | all-reduce | flops 1 | bytes 8 | tf_op jit(solution)/shard_map/psum | solution.py:123
  72.6 1.3 collective-permute-start.8
  73.9 5.1 %collective-permute-start.9 = (f32[1]{0:T(128)}, f32[1]{0:T(128)}, u32[]{:S(2)}, u32[]{:S(2)}) collective-permute-start(f32[1]{0:T(128)} %get-tuple-element.167), channel_id=1, source_target_pairs={{0,4},{4,8},{8,12},{12,16},{16,20},{20,24},{24,28},{1,5},{5,9},{9,... | collective-permute-start | bytes 20 | tf_op jit(solution)/shard_map/ppermute | solution.py:24
  80.0 1.3 pad_maximum_fusion.100
  87.6 1.1 collective-permute-done.10
  88.7 1.5 collective-permute-start.11
  90.3 2.1 collective-permute-done.11
  93.0 1.3 pad_maximum_fusion.108
  94.3 19.3 %psum.36 = f32[2]{0:T(128)S(1)} all-reduce(f32[2]{0:T(128)S(1)} %pad_maximum_fusion.108), channel_id=1, replica_groups=mesh['macro'=8,'rep'=4] {'macro'}, use_global_device_ids=true, to_apply=%region_7.0 | all-reduce | flops 2 | bytes 16 | tf_op jit(solution)/shard_map/psum | solution.py:123
  117.5 1.3 collective-permute-start.12
  118.8 5.1 %collective-permute-start.13 = (f32[1]{0:T(128)}, f32[1]{0:T(128)}, u32[]{:S(2)}, u32[]{:S(2)}) collective-permute-start(f32[1]{0:T(128)} %get-tuple-element.163), channel_id=1, source_target_pairs={{0,4},{4,8},{8,12},{12,16},{16,20},{20,24},{24,28},{1,5},{5,9},{9,... | collective-permute-start | bytes 20 | tf_op jit(solution)/shard_map/ppermute | solution.py:24
  124.7 1.4 pad_maximum_fusion.102
  132.4 1.1 collective-permute-done.14
  133.5 1.5 collective-permute-start.15
  135.0 2.1 collective-permute-done.15
  137.8 1.9 pad_maximum_fusion.109
  139.7 19.3 %psum.37 = f32[3]{0:T(128)S(1)} all-reduce(f32[3]{0:T(128)S(1)} %pad_maximum_fusion.109), channel_id=1, replica_groups=mesh['macro'=8,'rep'=4] {'macro'}, use_global_device_ids=true, to_apply=%region_12.0 | all-reduce | flops 3 | bytes 24 | tf_op jit(solution)/shard_map/psum | solution.py:123
  161.7 1.3 multiply_add_fusion.3
  163.7 1.3 collective-permute-start.16
  165.0 5.1 %collective-permute-start.17 = (f32[1]{0:T(128)}, f32[1]{0:T(128)}, u32[]{:S(2)}, u32[]{:S(2)}) collective-permute-start(f32[1]{0:T(128)} %get-tuple-element.159), channel_id=1, source_target_pairs={{0,4},{4,8},{8,12},{12,16},{16,20},{20,24},{24,28},{1,5},{5,9},{9,... | collective-permute-start | bytes 20 | tf_op jit(solution)/shard_map/ppermute | solution.py:24
  170.9 1.3 pad_maximum_fusion.104
  178.5 1.1 collective-permute-done.18
  179.6 1.5 collective-permute-start.19
  181.1 2.1 collective-permute-done.19
  183.9 2.6 pad_maximum_fusion.110
  186.5 19.3 %psum.38 = f32[4]{0:T(128)S(1)} all-reduce(f32[4]{0:T(128)S(1)} %pad_maximum_fusion.110), channel_id=1, replica_groups=mesh['macro'=8,'rep'=4] {'macro'}, use_global_device_ids=true, to_apply=%region_19.0 | all-reduce | flops 4 | bytes 32 | tf_op jit(solution)/shard_map/psum | solution.py:123
  208.6 1.9 multiply_add_fusion.2
  211.2 1.3 collective-permute-start.20
  212.5 5.1 %collective-permute-start.21 = (f32[1]{0:T(128)}, f32[1]{0:T(128)}, u32[]{:S(2)}, u32[]{:S(2)}) collective-permute-start(f32[1]{0:T(128)} %get-tuple-element.155), channel_id=1, source_target_pairs={{0,4},{4,8},{8,12},{12,16},{16,20},{20,24},{24,28},{1,5},{5,9},{9,... | collective-permute-start | bytes 20 | tf_op jit(solution)/shard_map/ppermute | solution.py:24
  218.4 1.3 pad_maximum_fusion.106
  226.0 1.1 collective-permute-done.22
  227.1 1.5 collective-permute-start.23
  237.9 3.2 %stack.71 = f32[5]{0:T(128)S(1)} concatenate(f32[1]{0:T(128)} %bitcast.30, f32[1]{0:T(128)} %bitcast.31, f32[1]{0:T(128)} %bitcast.32, f32[1]{0:T(128)} %bitcast.33, f32[1]{0:T(128)} %bitcast.34), dimensions={0} | concatenate | bytes 40 | tf_op jit(solution)/shard_map/stack | solution.py:137
  241.2 19.3 %psum.39 = f32[5]{0:T(128)S(1)} all-reduce(f32[5]{0:T(128)S(1)} %stack.71), channel_id=1, replica_groups=mesh['macro'=8,'rep'=4] {'macro'}, use_global_device_ids=true, to_apply=%region_27.0 | all-reduce | flops 5 | bytes 40 | tf_op jit(solution)/shard_map/psum | solution.py:123
  (175 shorter events, 55.1 us)
Async XLA Ops:
  1.4 7.5 %copy-start.3 = (f32[512]{0:T(512)S(1)}, f32[512]{0:T(512)}, u32[]{:S(2)}) copy-start(f32[512]{0:T(512)} %param.5) | copy-start | bytes 6148
  1.4 7.5 %collective-permute-start = (f32[1]{0:T(128)}, f32[1]{0:T(128)}, u32[]{:S(2)}, u32[]{:S(2)}) collective-permute-start(f32[1]{0:T(128)} %get-tuple-element.174), channel_id=1, source_target_pairs={{4,0},{8,4},{12,8},{16,12},{20,16},{24,20},{28,24},{5,1},{9,5},{13... | collective-permute-start | bytes 20 | tf_op jit(solution)/shard_map/ppermute | solution.py:26
  2.8 7.0 %collective-permute-start.1 = (f32[1]{0:T(128)}, f32[1]{0:T(128)}, u32[]{:S(2)}, u32[]{:S(2)}) collective-permute-start(f32[1]{0:T(128)} %get-tuple-element.175), channel_id=1, source_target_pairs={{0,4},{4,8},{8,12},{12,16},{16,20},{20,24},{24,28},{1,5},{5,9},{9,... | collective-permute-start | bytes 20 | tf_op jit(solution)/shard_map/ppermute | solution.py:24
  8.9 0.9 copy-start.2
  12.7 1.0 copy-start
  13.0 0.7 copy-start.1
  19.1 1.2 collective-permute-start.2
  20.3 3.6 %collective-permute-start.3 = (f32[512]{0:T(512)S(1)}, f32[512]{0:T(512)S(1)}, u32[]{:S(2)}, u32[]{:S(2)}) collective-permute-start(f32[512]{0:T(512)S(1)} %add.1256), channel_id=1, source_target_pairs={{0,2},{1,3},{2,0},{3,1},{4,6},{5,7},{6,4},{7,5},{8,10},{9,11},{10,... | collective-permute-start | bytes 6152 | tf_op jit(solution)/shard_map/ppermute | solution.py:116
  24.5 7.3 %collective-permute-start.4 = (f32[1]{0:T(128)}, f32[1]{0:T(128)}, u32[]{:S(2)}, u32[]{:S(2)}) collective-permute-start(f32[1]{0:T(128)} %get-tuple-element.170), channel_id=1, source_target_pairs={{4,0},{8,4},{12,8},{16,12},{20,16},{24,20},{28,24},{5,1},{9,5},{13... | collective-permute-start | bytes 20 | tf_op jit(solution)/shard_map/ppermute | solution.py:26
  25.8 6.9 %collective-permute-start.5 = (f32[1]{0:T(128)}, f32[1]{0:T(128)}, u32[]{:S(2)}, u32[]{:S(2)}) collective-permute-start(f32[1]{0:T(128)} %get-tuple-element.171), channel_id=1, source_target_pairs={{0,4},{4,8},{8,12},{12,16},{16,20},{20,24},{24,28},{1,5},{5,9},{9,... | collective-permute-start | bytes 20 | tf_op jit(solution)/shard_map/ppermute | solution.py:24
  40.3 1.2 collective-permute-start.6
  41.5 3.6 %collective-permute-start.7 = (f32[512]{0:T(512)S(1)}, f32[512]{0:T(512)S(1)}, u32[]{:S(2)}, u32[]{:S(2)}) collective-permute-start(f32[512]{0:T(512)S(1)} %add.1291), channel_id=1, source_target_pairs={{0,2},{1,3},{2,0},{3,1},{4,6},{5,7},{6,4},{7,5},{8,10},{9,11},{10,... | collective-permute-start | bytes 6152 | tf_op jit(solution)/shard_map/ppermute | solution.py:116
  72.6 6.4 %collective-permute-start.8 = (f32[1]{0:T(128)}, f32[1]{0:T(128)}, u32[]{:S(2)}, u32[]{:S(2)}) collective-permute-start(f32[1]{0:T(128)} %get-tuple-element.166), channel_id=1, source_target_pairs={{4,0},{8,4},{12,8},{16,12},{20,16},{24,20},{28,24},{5,1},{9,5},{13... | collective-permute-start | bytes 20 | tf_op jit(solution)/shard_map/ppermute | solution.py:26
  73.9 6.0 %collective-permute-start.9 = (f32[1]{0:T(128)}, f32[1]{0:T(128)}, u32[]{:S(2)}, u32[]{:S(2)}) collective-permute-start(f32[1]{0:T(128)} %get-tuple-element.167), channel_id=1, source_target_pairs={{0,4},{4,8},{8,12},{12,16},{16,20},{20,24},{24,28},{1,5},{5,9},{9,... | collective-permute-start | bytes 20 | tf_op jit(solution)/shard_map/ppermute | solution.py:24
  87.5 1.2 collective-permute-start.10
  88.7 3.6 %collective-permute-start.11 = (f32[512]{0:T(512)S(1)}, f32[512]{0:T(512)S(1)}, u32[]{:S(2)}, u32[]{:S(2)}) collective-permute-start(f32[512]{0:T(512)S(1)} %add.1326), channel_id=1, source_target_pairs={{0,2},{1,3},{2,0},{3,1},{4,6},{5,7},{6,4},{7,5},{8,10},{9,11},{10,... | collective-permute-start | bytes 6152 | tf_op jit(solution)/shard_map/ppermute | solution.py:116
  117.5 6.4 %collective-permute-start.12 = (f32[1]{0:T(128)}, f32[1]{0:T(128)}, u32[]{:S(2)}, u32[]{:S(2)}) collective-permute-start(f32[1]{0:T(128)} %get-tuple-element.162), channel_id=1, source_target_pairs={{4,0},{8,4},{12,8},{16,12},{20,16},{24,20},{28,24},{5,1},{9,5},{13... | collective-permute-start | bytes 20 | tf_op jit(solution)/shard_map/ppermute | solution.py:26
  118.8 5.9 %collective-permute-start.13 = (f32[1]{0:T(128)}, f32[1]{0:T(128)}, u32[]{:S(2)}, u32[]{:S(2)}) collective-permute-start(f32[1]{0:T(128)} %get-tuple-element.163), channel_id=1, source_target_pairs={{0,4},{4,8},{8,12},{12,16},{16,20},{20,24},{24,28},{1,5},{5,9},{9,... | collective-permute-start | bytes 20 | tf_op jit(solution)/shard_map/ppermute | solution.py:24
  132.3 1.2 collective-permute-start.14
  133.5 3.6 %collective-permute-start.15 = (f32[512]{0:T(512)S(1)}, f32[512]{0:T(512)S(1)}, u32[]{:S(2)}, u32[]{:S(2)}) collective-permute-start(f32[512]{0:T(512)S(1)} %add.1362), channel_id=1, source_target_pairs={{0,2},{1,3},{2,0},{3,1},{4,6},{5,7},{6,4},{7,5},{8,10},{9,11},{10,... | collective-permute-start | bytes 6152 | tf_op jit(solution)/shard_map/ppermute | solution.py:116
  163.7 6.4 %collective-permute-start.16 = (f32[1]{0:T(128)}, f32[1]{0:T(128)}, u32[]{:S(2)}, u32[]{:S(2)}) collective-permute-start(f32[1]{0:T(128)} %get-tuple-element.158), channel_id=1, source_target_pairs={{4,0},{8,4},{12,8},{16,12},{20,16},{24,20},{28,24},{5,1},{9,5},{13... | collective-permute-start | bytes 20 | tf_op jit(solution)/shard_map/ppermute | solution.py:26
  165.0 5.9 %collective-permute-start.17 = (f32[1]{0:T(128)}, f32[1]{0:T(128)}, u32[]{:S(2)}, u32[]{:S(2)}) collective-permute-start(f32[1]{0:T(128)} %get-tuple-element.159), channel_id=1, source_target_pairs={{0,4},{4,8},{8,12},{12,16},{16,20},{20,24},{24,28},{1,5},{5,9},{9,... | collective-permute-start | bytes 20 | tf_op jit(solution)/shard_map/ppermute | solution.py:24
  178.4 1.2 collective-permute-start.18
  179.6 3.6 %collective-permute-start.19 = (f32[512]{0:T(512)S(1)}, f32[512]{0:T(512)S(1)}, u32[]{:S(2)}, u32[]{:S(2)}) collective-permute-start(f32[512]{0:T(512)S(1)} %add.1400), channel_id=1, source_target_pairs={{0,2},{1,3},{2,0},{3,1},{4,6},{5,7},{6,4},{7,5},{8,10},{9,11},{10,... | collective-permute-start | bytes 6152 | tf_op jit(solution)/shard_map/ppermute | solution.py:116
  211.2 6.4 %collective-permute-start.20 = (f32[1]{0:T(128)}, f32[1]{0:T(128)}, u32[]{:S(2)}, u32[]{:S(2)}) collective-permute-start(f32[1]{0:T(128)} %get-tuple-element.154), channel_id=1, source_target_pairs={{4,0},{8,4},{12,8},{16,12},{20,16},{24,20},{28,24},{5,1},{9,5},{13... | collective-permute-start | bytes 20 | tf_op jit(solution)/shard_map/ppermute | solution.py:26
  212.5 5.9 %collective-permute-start.21 = (f32[1]{0:T(128)}, f32[1]{0:T(128)}, u32[]{:S(2)}, u32[]{:S(2)}) collective-permute-start(f32[1]{0:T(128)} %get-tuple-element.155), channel_id=1, source_target_pairs={{0,4},{4,8},{8,12},{12,16},{16,20},{20,24},{24,28},{1,5},{5,9},{9,... | collective-permute-start | bytes 20 | tf_op jit(solution)/shard_map/ppermute | solution.py:24
  225.9 1.2 collective-permute-start.22
  227.1 10.1 %collective-permute-start.23 = (f32[512]{0:T(512)S(1)}, f32[512]{0:T(512)S(1)}, u32[]{:S(2)}, u32[]{:S(2)}) collective-permute-start(f32[512]{0:T(512)S(1)} %add.1439), channel_id=1, source_target_pairs={{0,2},{1,3},{2,0},{3,1},{4,6},{5,7},{6,4},{7,5},{8,10},{9,11},{10,... | collective-permute-start | bytes 6152 | tf_op jit(solution)/shard_map/ppermute | solution.py:116
